TPU v7x, 32 devices: a whole 2x2x4 slice. The times are simulated.
32 devices in a mesh: section: 4 (over y, x), tensor: 8 (over z, core).
Axes of the slice: x: 2, y: 2, z: 4, core: 2. Of those that a mesh axis runs over, the one named last changes fastest.
Arguments:
- token_ids: int32 [3, 48], replicated, may hold values from 0 to 31999
- emb_table: bfloat16 [32000, 4096], P('section', 'tensor'), may hold values from -6 to 6
- attn_gain: bfloat16 [4, 4096], P('section'), may hold values from 0.25 to 1.75
- query_weight: bfloat16 [4, 4096, 4096], P('section', None, 'tensor'), may hold values from -8 to 8
- key_weight: bfloat16 [4, 4096, 4096], P('section', None, 'tensor'), may hold values from -8 to 8
- value_weight: bfloat16 [4, 4096, 4096], P('section', None, 'tensor'), may hold values from -0.09375 to 0.09375
- mix_weight: float32 [4, 32], P('section', 'tensor'), may hold values from 0.2 to 0.8
- out_weight: bfloat16 [4, 4096, 4096], P('section', 'tensor'), may hold values from -0.125 to 0.125
Outputs:
- layer_outputs: bfloat16 [4, 3, 48, 4096], P('section', None, None, 'tensor')
All inputs are finite; a program needn't handle non-finite values.
Results may differ from a plain program's by a relative error of at most 0.033.
Values may be sent and summed in bfloat16 or wider, within the bound.
A program may use at most 64 MiB of HBM per device.

v0:
```python
import jax
import jax.numpy as jnp
from jax import lax
from jax.sharding import PartitionSpec as P

EPSILON = 1e-05
ROTARY_BASE = 10000.0


def broadcast(array, axis, root):
    mine = lax.axis_index(axis) == root
    return lax.psum(jnp.where(mine, array, jnp.zeros_like(array)), axis)


def shifted(value, axis, steps):
    count = lax.axis_size(axis)
    first, last = (max(0, -steps), min(count, count - steps))
    return lax.ppermute(value, axis, [(source, source + steps) for source in range(first, last)])


def rms_scale(values, norm_gain):
    mean_square = jnp.mean(values * values, axis=-1, keepdims=True)
    return values * lax.rsqrt(mean_square + EPSILON) * norm_gain


def rotate(values):
    length = values.shape[-3]
    head_dim = values.shape[-1]
    half_dim = head_dim // 2
    positions = jnp.arange(length, dtype=jnp.float32)
    frequency = ROTARY_BASE ** (-(jnp.arange(half_dim, dtype=jnp.float32) * 2.0) / head_dim)
    angles = positions[:, None] * frequency[None, :]
    cosine = jnp.cos(angles)[:, None, :]
    sine_table = jnp.sin(angles)[:, None, :]
    leading = values[..., :half_dim]
    second = values[..., half_dim:]
    return jnp.concatenate(
        [leading * cosine - second * sine_table, second * cosine + leading * sine_table], axis=-1
    )


def attend(queries, key_rows, mixed_values):
    length = queries.shape[0]
    head_dim = queries.shape[2]
    scores = jnp.einsum(
        "qhd,khd->hqk", queries, key_rows, preferred_element_type=jnp.float32
    ) * head_dim ** (-0.5)
    causal = jnp.arange(length)[:, None] >= jnp.arange(length)[None, :]
    scores = jnp.where(causal, scores, -1e30)
    row_top = jnp.max(scores, axis=-1, keepdims=True)
    expo = jnp.exp(scores - row_top)
    attn_probs = (expo / jnp.sum(expo, axis=-1, keepdims=True)).astype(jnp.bfloat16)
    attended = jnp.einsum(
        "hqk,khd->qhd", attn_probs, mixed_values, preferred_element_type=jnp.float32
    )
    return attended.astype(jnp.bfloat16)


def shards(
    token_ids, emb_table, attn_gain, query_weight, key_weight, value_weight, mix_weight, out_weight
):
    section_rank = lax.axis_index("section")
    section_count = lax.axis_size("section")
    batches, length = token_ids.shape
    vocab_local, width_local = emb_table.shape
    head_local = mix_weight.shape[1]
    head_dim = query_weight.shape[2] // head_local
    norm_gain = attn_gain[0].astype(jnp.float32)
    w_query = query_weight[0]
    w_key = key_weight[0]
    w_value = value_weight[0]
    w_out = out_weight[0]
    mix_rate = mix_weight[0][None, :, None]
    flat_ids = token_ids.reshape(-1) - section_rank * vocab_local
    one_hot = (flat_ids[:, None] == jnp.arange(vocab_local, dtype=jnp.int32)[None, :]).astype(
        jnp.bfloat16
    )
    looked = jnp.dot(one_hot, emb_table, preferred_element_type=jnp.float32)
    first_shard = lax.psum(looked.astype(jnp.bfloat16), "section")
    first_full = lax.all_gather(first_shard, "tensor", axis=1, tiled=True)
    first_float = first_full.astype(jnp.float32)

    def root_project():
        first_norm = rms_scale(first_float, norm_gain).astype(jnp.bfloat16)
        return jnp.dot(first_norm, w_value, preferred_element_type=jnp.float32).astype(jnp.bfloat16)

    def skipped():
        return jnp.zeros((first_full.shape[0], w_value.shape[1]), jnp.bfloat16)

    own_values = lax.cond(section_rank == 0, root_project, skipped)
    first_values = broadcast(own_values, "section", 0)
    source_values = first_values.reshape(batches, length, head_local, head_dim)
    first_blocks = first_shard.reshape(batches, length, width_local)

    def attention_branch(full_rows, micro_index):
        normed = rms_scale(full_rows.astype(jnp.float32), norm_gain).astype(jnp.bfloat16)
        queries = jnp.dot(normed, w_query, preferred_element_type=jnp.float32)
        key_rows = jnp.dot(normed, w_key, preferred_element_type=jnp.float32)
        values = jnp.dot(normed, w_value, preferred_element_type=jnp.float32)
        queries = rotate(queries.reshape(length, head_local, head_dim)).astype(jnp.bfloat16)
        key_rows = rotate(key_rows.reshape(length, head_local, head_dim)).astype(jnp.bfloat16)
        values = values.reshape(length, head_local, head_dim)
        picked = lax.dynamic_index_in_dim(source_values, micro_index, 0, keepdims=False).astype(
            jnp.float32
        )
        mixed_values = (mix_rate * values + (1.0 - mix_rate) * picked).astype(jnp.bfloat16)
        attended = attend(queries, key_rows, mixed_values).reshape(length, head_local * head_dim)
        return jnp.dot(attended, w_out, preferred_element_type=jnp.float32)

    def advance(step_index, loop_state):
        incoming, outputs = loop_state
        position = step_index - section_rank
        is_valid = (position >= 0) & (position < batches)
        micro_index = jnp.clip(position, 0, batches - 1)
        starting = lax.dynamic_index_in_dim(first_blocks, micro_index, 0, keepdims=False)
        shard_rows = jnp.where(section_rank == 0, starting, incoming)
        full_rows = lax.all_gather(shard_rows, "tensor", axis=1, tiled=True)
        summed = lax.psum_scatter(
            attention_branch(full_rows, micro_index).astype(jnp.bfloat16),
            "tensor",
            scatter_dimension=1,
            tiled=True,
        ).astype(jnp.float32)
        fresh_rows = (shard_rows.astype(jnp.float32) + summed).astype(jnp.bfloat16)
        previous = lax.dynamic_index_in_dim(outputs, micro_index, 0, keepdims=False)
        kept_rows = jnp.where(is_valid, fresh_rows, previous)
        outputs = lax.dynamic_update_index_in_dim(outputs, kept_rows, micro_index, 0)
        incoming = shifted(fresh_rows, "section", 1)
        return (incoming, outputs)

    incoming = jnp.zeros((length, width_local), jnp.bfloat16)
    outputs = jnp.zeros((batches, length, width_local), jnp.bfloat16)
    step_count = batches + section_count - 1
    incoming, outputs = lax.fori_loop(0, step_count, advance, (incoming, outputs))
    return outputs[None]


def solution(mesh):
    in_specs = (
        P(),
        P("section", "tensor"),
        P("section", None),
        P("section", None, "tensor"),
        P("section", None, "tensor"),
        P("section", None, "tensor"),
        P("section", "tensor"),
        P("section", "tensor", None),
    )
    out_specs = P("section", None, None, "tensor")
    return jax.shard_map(shards, mesh=mesh, in_specs=in_specs, out_specs=out_specs, check_vma=False)
```

profile of v0, /device:TPU:6, one launch (start us, length us, event | category | flops | bytes accessed | tf_op | source)
XLA Modules:
  0.0 535.6 jit_solution(17182920479941421456)
XLA Ops:
  7.3 5.4 %fusion.49 = bf16[144,512]{1,0:T(8,128)(2,1)} fusion(bf16[8000,512]{1,0:T(8,128)(2,1)} %param.13, s32[144]{0:T(256)S(1)} %sub.74), kind=kOutput, calls=%fused_computation.65 | convolution fusion | flops 1180873728 | bytes 8340032 | tf_op jit(solution)/shard_map/dot_general | solution.py:78
  12.8 42.8 %all-reduce.3.cloned.1.call-done = bf16[144,512]{1,0:T(8,128)(2,1)} async-done(((bf16[144,512]{1,0:T(8,128)(2,1)}), bf16[144,512]{1,0:T(8,128)(2,1)}) %all-reduce.3.cloned.1.call-update) | async-done | bytes 147472 | tf_op jit(solution)/shard_map/psum | solution.py:79
  55.7 25.1 %all-gather.2.cloned.1.call-done = bf16[144,4096]{1,0:T(8,128)(2,1)} async-done(((bf16[144,512]{1,0:T(8,128)(2,1)}), bf16[144,4096]{1,0:T(8,128)(2,1)}) %all-gather.2.cloned.1.call-update) | async-done | bytes 1179664 | tf_op jit(solution)/shard_map/all_gather | solution.py:80
  83.1 42.9 %all-reduce.5.cloned.1.call-done = bf16[3,48,4,128]{3,2,1,0:T(4,128)(2,1)} async-done(((bf16[3,48,4,128]{3,2,1,0:T(4,128)(2,1)}), bf16[3,48,4,128]{3,2,1,0:T(4,128)(2,1)}) %all-reduce.5.cloned.1.call-update) | async-done | bytes 147472 | tf_op jit(solution)/shard_map/psum | solution.py:12
  126.1 402.3 %while.16 = (s32[]{:T(128)}, bf16[48,512]{1,0:T(8,128)(2,1)S(1)}, bf16[3,48,512]{2,1,0:T(8,128)(2,1)S(1)}, pred[]{:T(512)}, s32[]{:T(128)}, /*index=5*/bf16[3,48...) while((s32[]{:T(128)}, bf16[48,512]{1,0:T(8,128)(2,1)S(1)}, ...), condition=%wide.region_10.11_spmd, body=%wide.region_5.10_spmd.sunk | while | flops 813919744 | bytes 23199736 | solution.py:134
  127.0 14.5 %all_gather.13 = bf16[48,4096]{1,0:T(8,128)(2,1)S(1)} all-gather(bf16[48,512]{1,0:T(8,128)(2,1)S(1)} %bitcast_select_fusion.3), channel_id=1, replica_groups=mesh['section'=4,'tensor'=8] {'tensor'}, dimensions={1}, use_global_device_ids=true | all-gather | bytes 442368 | tf_op jit(solution)/shard_map/while/body/eval_jaxpr/all_gather | solution.py:117
  141.7 3.1 fusion.94
  152.7 3.8 convolution_convert_fusion.3
  156.5 32.1 %reduce-scatter.2.cloned.1.call-done = bf16[48,512]{1,0:T(8,128)(2,1)} async-done(((bf16[48,4096]{1,0:T(8,128)(2,1)}), bf16[48,512]{1,0:T(8,128)(2,1)}) %reduce-scatter.2.cloned.1.call-update) | async-done | bytes 49168 | tf_op jit(solution)/shard_map/while/body/eval_jaxpr/reduce_scatter | solution.py:118
  190.8 4.7 collective-permute-done
  196.3 14.4 %all_gather.13 = bf16[48,4096]{1,0:T(8,128)(2,1)S(1)} all-gather(bf16[48,512]{1,0:T(8,128)(2,1)S(1)} %bitcast_select_fusion.3), channel_id=1, replica_groups=mesh['section'=4,'tensor'=8] {'tensor'}, dimensions={1}, use_global_device_ids=true | all-gather | bytes 442368 | tf_op jit(solution)/shard_map/while/body/eval_jaxpr/all_gather | solution.py:117
  222.0 3.8 convolution_convert_fusion.3
  225.8 29.6 %reduce-scatter.2.cloned.1.call-done = bf16[48,512]{1,0:T(8,128)(2,1)} async-done(((bf16[48,4096]{1,0:T(8,128)(2,1)}), bf16[48,512]{1,0:T(8,128)(2,1)}) %reduce-scatter.2.cloned.1.call-update) | async-done | bytes 49168 | tf_op jit(solution)/shard_map/while/body/eval_jaxpr/reduce_scatter | solution.py:118
  257.5 4.7 collective-permute-done
  263.0 14.4 %all_gather.13 = bf16[48,4096]{1,0:T(8,128)(2,1)S(1)} all-gather(bf16[48,512]{1,0:T(8,128)(2,1)S(1)} %bitcast_select_fusion.3), channel_id=1, replica_groups=mesh['section'=4,'tensor'=8] {'tensor'}, dimensions={1}, use_global_device_ids=true | all-gather | bytes 442368 | tf_op jit(solution)/shard_map/while/body/eval_jaxpr/all_gather | solution.py:117
  277.7 3.1 fusion.94
  288.7 3.8 convolution_convert_fusion.3
  292.5 29.4 %reduce-scatter.2.cloned.1.call-done = bf16[48,512]{1,0:T(8,128)(2,1)} async-done(((bf16[48,4096]{1,0:T(8,128)(2,1)}), bf16[48,512]{1,0:T(8,128)(2,1)}) %reduce-scatter.2.cloned.1.call-update) | async-done | bytes 49168 | tf_op jit(solution)/shard_map/while/body/eval_jaxpr/reduce_scatter | solution.py:118
  324.0 4.7 collective-permute-done
  329.5 14.4 %all_gather.13 = bf16[48,4096]{1,0:T(8,128)(2,1)S(1)} all-gather(bf16[48,512]{1,0:T(8,128)(2,1)S(1)} %bitcast_select_fusion.3), channel_id=1, replica_groups=mesh['section'=4,'tensor'=8] {'tensor'}, dimensions={1}, use_global_device_ids=true | all-gather | bytes 442368 | tf_op jit(solution)/shard_map/while/body/eval_jaxpr/all_gather | solution.py:117
  355.2 3.8 convolution_convert_fusion.3
  359.0 29.5 %reduce-scatter.2.cloned.1.call-done = bf16[48,512]{1,0:T(8,128)(2,1)} async-done(((bf16[48,4096]{1,0:T(8,128)(2,1)}), bf16[48,512]{1,0:T(8,128)(2,1)}) %reduce-scatter.2.cloned.1.call-update) | async-done | bytes 49168 | tf_op jit(solution)/shard_map/while/body/eval_jaxpr/reduce_scatter | solution.py:118
  390.6 4.7 collective-permute-done
  396.1 14.4 %all_gather.13 = bf16[48,4096]{1,0:T(8,128)(2,1)S(1)} all-gather(bf16[48,512]{1,0:T(8,128)(2,1)S(1)} %bitcast_select_fusion.3), channel_id=1, replica_groups=mesh['section'=4,'tensor'=8] {'tensor'}, dimensions={1}, use_global_device_ids=true | all-gather | bytes 442368 | tf_op jit(solution)/shard_map/while/body/eval_jaxpr/all_gather | solution.py:117
  410.8 3.1 fusion.94
  421.8 3.8 convolution_convert_fusion.3
  425.6 29.4 %reduce-scatter.2.cloned.1.call-done = bf16[48,512]{1,0:T(8,128)(2,1)} async-done(((bf16[48,4096]{1,0:T(8,128)(2,1)}), bf16[48,512]{1,0:T(8,128)(2,1)}) %reduce-scatter.2.cloned.1.call-update) | async-done | bytes 49168 | tf_op jit(solution)/shard_map/while/body/eval_jaxpr/reduce_scatter | solution.py:118
  457.2 4.7 collective-permute-done
  462.7 14.5 %all_gather.13 = bf16[48,4096]{1,0:T(8,128)(2,1)S(1)} all-gather(bf16[48,512]{1,0:T(8,128)(2,1)S(1)} %bitcast_select_fusion.3), channel_id=1, replica_groups=mesh['section'=4,'tensor'=8] {'tensor'}, dimensions={1}, use_global_device_ids=true | all-gather | bytes 442368 | tf_op jit(solution)/shard_map/while/body/eval_jaxpr/all_gather | solution.py:117
  488.4 3.8 convolution_convert_fusion.3
  492.2 29.4 %reduce-scatter.2.cloned.1.call-done = bf16[48,512]{1,0:T(8,128)(2,1)} async-done(((bf16[48,4096]{1,0:T(8,128)(2,1)}), bf16[48,512]{1,0:T(8,128)(2,1)}) %reduce-scatter.2.cloned.1.call-update) | async-done | bytes 49168 | tf_op jit(solution)/shard_map/while/body/eval_jaxpr/reduce_scatter | solution.py:118
  523.7 4.7 collective-permute-done
  (151 shorter events, 79.4 us)
Async XLA Ops:
  6.5 49.1 %all-reduce.3.cloned.1.call-start = ((), (), s32[]{:S(2)}) async-start(), calls=%async_computation.1 | async-start | bytes 294912 | tf_op jit(solution)/shard_map/psum | solution.py:79
  7.3 48.4 %copy-start.1 = (bf16[1,4096]{1,0:T(2,128)(2,1)S(1)}, bf16[1,4096]{1,0:T(2,128)(2,1)}, u32[]{:S(2)}) copy-start(bf16[1,4096]{1,0:T(2,128)(2,1)} %param.14) | copy-start | bytes 24580
  12.8 68.0 %all-gather.2.cloned.1.call-start = ((), (), s32[]{:S(2)}) async-start(), calls=%async_computation.2 | async-start | bytes 1327104 | tf_op jit(solution)/shard_map/all_gather | solution.py:80
  55.6 70.4 %all-reduce.5.cloned.1.call-start = ((), (), s32[]{:S(2)}) async-start(), calls=%async_computation.3 | async-start | bytes 294912 | tf_op jit(solution)/shard_map/psum | solution.py:12
  82.3 43.8 %copy-start.2 = (f32[1,4]{1,0:T(1,128)S(1)}, f32[1,4]{1,0:T(1,128)}, u32[]{:S(2)}) copy-start(f32[1,4]{1,0:T(1,128)} %param.18) | copy-start | bytes 52
  126.1 62.5 %reduce-scatter.2.cloned.1.call-start = ((), (), s32[]{:S(2)}) async-start(), calls=%async_computation.4 | async-start | bytes 442368 | tf_op jit(solution)/shard_map/while/body/eval_jaxpr/reduce_scatter | solution.py:118
  189.5 6.0 %collective-permute-start = (bf16[48,512]{1,0:T(8,128)(2,1)S(1)}, bf16[48,512]{1,0:T(8,128)(2,1)S(1)}, u32[]{:S(2)}, u32[]{:S(2)}) collective-permute-start(bf16[48,512]{1,0:T(8,128)(2,1)S(1)} %get-tuple-element.432), channel_id=1, source_target_pairs={{0,8},{8,16},{16,24},{1,9},{9,17},{17,25},{2,10},{10,18},{18,26},{... | collective-permute-start | bytes 147464 | tf_op jit(solution)/shard_map/while/body/eval_jaxpr/ppermute | solution.py:18
  195.5 59.9 %reduce-scatter.2.cloned.1.call-start = ((), (), s32[]{:S(2)}) async-start(), calls=%async_computation.4 | async-start | bytes 442368 | tf_op jit(solution)/shard_map/while/body/eval_jaxpr/reduce_scatter | solution.py:118
  256.2 6.0 %collective-permute-start = (bf16[48,512]{1,0:T(8,128)(2,1)S(1)}, bf16[48,512]{1,0:T(8,128)(2,1)S(1)}, u32[]{:S(2)}, u32[]{:S(2)}) collective-permute-start(bf16[48,512]{1,0:T(8,128)(2,1)S(1)} %get-tuple-element.432), channel_id=1, source_target_pairs={{0,8},{8,16},{16,24},{1,9},{9,17},{17,25},{2,10},{10,18},{18,26},{... | collective-permute-start | bytes 147464 | tf_op jit(solution)/shard_map/while/body/eval_jaxpr/ppermute | solution.py:18
  262.2 59.7 %reduce-scatter.2.cloned.1.call-start = ((), (), s32[]{:S(2)}) async-start(), calls=%async_computation.4 | async-start | bytes 442368 | tf_op jit(solution)/shard_map/while/body/eval_jaxpr/reduce_scatter | solution.py:118
  322.7 6.0 %collective-permute-start = (bf16[48,512]{1,0:T(8,128)(2,1)S(1)}, bf16[48,512]{1,0:T(8,128)(2,1)S(1)}, u32[]{:S(2)}, u32[]{:S(2)}) collective-permute-start(bf16[48,512]{1,0:T(8,128)(2,1)S(1)} %get-tuple-element.432), channel_id=1, source_target_pairs={{0,8},{8,16},{16,24},{1,9},{9,17},{17,25},{2,10},{10,18},{18,26},{... | collective-permute-start | bytes 147464 | tf_op jit(solution)/shard_map/while/body/eval_jaxpr/ppermute | solution.py:18
  328.7 59.8 %reduce-scatter.2.cloned.1.call-start = ((), (), s32[]{:S(2)}) async-start(), calls=%async_computation.4 | async-start | bytes 442368 | tf_op jit(solution)/shard_map/while/body/eval_jaxpr/reduce_scatter | solution.py:118
  389.3 6.0 %collective-permute-start = (bf16[48,512]{1,0:T(8,128)(2,1)S(1)}, bf16[48,512]{1,0:T(8,128)(2,1)S(1)}, u32[]{:S(2)}, u32[]{:S(2)}) collective-permute-start(bf16[48,512]{1,0:T(8,128)(2,1)S(1)} %get-tuple-element.432), channel_id=1, source_target_pairs={{0,8},{8,16},{16,24},{1,9},{9,17},{17,25},{2,10},{10,18},{18,26},{... | collective-permute-start | bytes 147464 | tf_op jit(solution)/shard_map/while/body/eval_jaxpr/ppermute | solution.py:18
  395.3 59.8 %reduce-scatter.2.cloned.1.call-start = ((), (), s32[]{:S(2)}) async-start(), calls=%async_computation.4 | async-start | bytes 442368 | tf_op jit(solution)/shard_map/while/body/eval_jaxpr/reduce_scatter | solution.py:118
  455.9 6.0 %collective-permute-start = (bf16[48,512]{1,0:T(8,128)(2,1)S(1)}, bf16[48,512]{1,0:T(8,128)(2,1)S(1)}, u32[]{:S(2)}, u32[]{:S(2)}) collective-permute-start(bf16[48,512]{1,0:T(8,128)(2,1)S(1)} %get-tuple-element.432), channel_id=1, source_target_pairs={{0,8},{8,16},{16,24},{1,9},{9,17},{17,25},{2,10},{10,18},{18,26},{... | collective-permute-start | bytes 147464 | tf_op jit(solution)/shard_map/while/body/eval_jaxpr/ppermute | solution.py:18
  461.9 59.7 %reduce-scatter.2.cloned.1.call-start = ((), (), s32[]{:S(2)}) async-start(), calls=%async_computation.4 | async-start | bytes 442368 | tf_op jit(solution)/shard_map/while/body/eval_jaxpr/reduce_scatter | solution.py:118
  522.4 6.0 %collective-permute-start = (bf16[48,512]{1,0:T(8,128)(2,1)S(1)}, bf16[48,512]{1,0:T(8,128)(2,1)S(1)}, u32[]{:S(2)}, u32[]{:S(2)}) collective-permute-start(bf16[48,512]{1,0:T(8,128)(2,1)S(1)} %get-tuple-element.432), channel_id=1, source_target_pairs={{0,8},{8,16},{16,24},{1,9},{9,17},{17,25},{2,10},{10,18},{18,26},{... | collective-permute-start | bytes 147464 | tf_op jit(solution)/shard_map/while/body/eval_jaxpr/ppermute | solution.py:18
  528.4 0.7 copy-start
Sparse Core Ops, SparseCore 0:
  12.9 42.6 all-reduce.2
  57.2 23.5 all-gather.1
  83.7 42.2 all-reduce.4
  156.6 31.9 reduce-scatter.1
  225.9 29.4 reduce-scatter.1
  292.6 29.2 reduce-scatter.1
  359.1 29.3 reduce-scatter.1
  425.7 29.2 reduce-scatter.1
  492.3 29.2 reduce-scatter.1
where the time goes:
time: 539 us; the launch traced here: 536 us
  waiting for transfers between devices  318 us (59%)
  blocking collectives  86.7 us (16%)
  matrix products  86.3 us (16%)
  other arithmetic  14.3 us (3%)
  between operations  13.2 us (2%)
  local copies, waits for them, and re-layouts  8.01 us (1%)
  starting transfers between devices  7.89 us (1%)
    reduce_scatter x6, waiting for transfers between devices, advance(): lax.psum_scatter(attention_branch(full_rows, micro_index).astype(jnp.bflo...  179 us
    all_gather x6, blocking collectives, advance(): full_rows = lax.all_gather(shard_rows, 'tensor', axis=1, tiled=True)  86.7 us
    psum x1, waiting for transfers between devices, broadcast(): return lax.psum(jnp.where(mine, array, jnp.zeros_like(array)), axis)  42.9 us
    psum x1, waiting for transfers between devices, shards(): first_shard = lax.psum(looked.astype(jnp.bfloat16), 'section')  42.8 us
    ppermute x6, waiting for transfers between devices, shifted(): lax.ppermute(value, axis, [(source, source + steps) for source in range(f...  28.1 us
    all_gather x1, waiting for transfers between devices, shards(): first_full = lax.all_gather(first_shard, 'tensor', axis=1, tiled=True)  25.1 us
    dot_general x6, matrix products, attention_branch(): return jnp.dot(attended, w_out, preferred_element_type=jnp.float32)  22.7 us
    dot_general x6, matrix products, attention_branch(): queries = jnp.dot(normed, w_query, preferred_element_type=jnp.float32)  18.4 us
  transfers between devices with their start and end apart: 15, of which 15 were waited for; matrix products, arithmetic and copies ran while one was open for 0% of the time, Pallas kernels for 0%

commit v1 on v0

v1 whole, which is shorter than its diff:
```python
import functools

import jax
import jax.numpy as jnp
from jax import lax
from jax.experimental import pallas as pl
from jax.experimental.pallas import tpu as pltpu
from jax.sharding import PartitionSpec as P

EPSILON = 1e-05
ROTARY_BASE = 10000.0
MESH = pl.DeviceIdType.MESH
F32 = jnp.float32
BF16 = jnp.bfloat16


def relay(
    dims,
    looked, gain, cosine, sine, mix, q_hbm, k_hbm, v_hbm, o_hbm,
    out,
    wq, wk, wv, wo, lk, full, fv, part, sib, pair, zr, hid, acc, att,
    w_sem, lk_s, lk_r, ag_s, ag_r, fw_s, fw_r, fv_s, fv_r, sp_s, sp_r, zs_s, zs_r, hp_s,
):
    S, T, B, L, W, heads, head_dim = dims
    Z = T // 2
    width = heads * head_dim
    sec = lax.axis_index("section")
    ten = lax.axis_index("tensor")
    z = lax.div(ten, 2)
    c = lax.rem(ten, 2)
    other = 1 - c
    mate = 2 * z + other
    root = sec == 0
    has_next = sec < S - 1

    def peer(d):
        return lax.rem(z + d, Z)

    def remote(src, dst, send, recv, to_sec, to_ten):
        return pltpu.make_async_remote_copy(
            src_ref=src, dst_ref=dst, send_sem=send, recv_sem=recv,
            device_id=(to_sec, to_ten), device_id_type=MESH,
        )

    def arrived(ref, send, recv):
        remote(ref, ref, send, recv, sec, mate).wait_recv()

    def sent(ref, send, recv):
        remote(ref, ref, send, recv, sec, mate).wait_send()

    loads = [
        pltpu.make_async_copy(hbm.at[0], vmem, w_sem.at[i])
        for i, (hbm, vmem) in enumerate(((q_hbm, wq), (k_hbm, wk), (v_hbm, wv), (o_hbm, wo)))
    ]
    for load in loads:
        load.start()

    barrier = pltpu.get_barrier_semaphore()

    def greet(to_sec, to_ten):
        pl.semaphore_signal(barrier, inc=1, device_id=(to_sec, to_ten), device_id_type=MESH)

    greet(sec, mate)
    for d in range(1, Z):
        greet(sec, 2 * peer(d) + c)

    @pl.when(has_next)
    def _():
        for d in range(Z):
            greet(sec + 1, 2 * peer(d) + c)

    @pl.when(sec > 0)
    def _():
        for d in range(Z):
            greet(sec - 1, 2 * peer(d) + c)
        greet(0, ten)

    @pl.when(root)
    def _():
        for s in range(1, S):
            greet(s, ten)

    greeted = Z + jnp.where(has_next, Z, 0) + jnp.where(root, S - 1, Z + 1)
    pl.semaphore_wait(barrier, greeted)

    @pl.when(sec > 0)
    def _():
        for m in range(B):
            remote(
                looked.at[m], lk.at[m, sec - 1], lk_s.at[m], lk_r.at[m, sec - 1], 0, ten
            ).start()

    @pl.when(root)
    def _():
        for m in range(B):
            rows = looked[m].astype(F32)
            for s in range(S - 1):
                arrived(lk.at[m, s], lk_s.at[m], lk_r.at[m, s])
                rows = rows + lk[m, s].astype(F32)
            full[m, ten] = rows.astype(BF16)
            for d in range(1, Z):
                remote(
                    full.at[m, ten], full.at[m, ten], ag_s.at[m, d], ag_r.at[m, z],
                    sec, 2 * peer(d) + c,
                ).start()

    for load in loads[:3]:
        load.wait()

    def micro(m, carry):
        def block(t, square, first):
            rows = full[m, t].astype(F32)
            span = pl.ds(pl.multiple_of(t * W, W), W)
            scaled = (rows * gain[:, span]).astype(BF16)
            for i, weight in enumerate((wq, wk, wv)):
                product = jnp.dot(scaled, weight[span, :], preferred_element_type=F32)
                if first:
                    acc[i] = product
                else:
                    acc[i] += product
            return square + jnp.sum(rows * rows, axis=-1, keepdims=True)

        square = jnp.zeros((L, 1), F32)
        for d in range(Z):
            from_z = peer(d)
            t = 2 * from_z + c
            if d == 0:
                @pl.when(sec > 0)
                def _():
                    arrived(full.at[m, t], fw_s.at[m, from_z], ag_r.at[m, from_z])
            else:
                arrived(full.at[m, t], fw_s.at[m, from_z], ag_r.at[m, from_z])
            remote(
                full.at[m, t], full.at[m, t], fw_s.at[m, from_z], fw_r.at[m, from_z], sec, mate
            ).start()
            square = block(t, square, d == 0)
        for d in range(Z):
            from_z = peer(d)
            t = 2 * from_z + other
            arrived(full.at[m, t], fw_s.at[m, from_z], fw_r.at[m, from_z])
            square = block(t, square, False)
        scale = lax.rsqrt(square * (1.0 / (T * W)) + EPSILON)

        @pl.when(root)
        def _():
            fv[m] = (acc[2] * scale).astype(BF16)

        @pl.when(sec > 0)
        def _():
            arrived(fv.at[m], fv_s.at[m], fv_r.at[m])

        @pl.when(has_next)
        def _():
            remote(fv.at[m], fv.at[m], fv_s.at[m], fv_r.at[m], sec + 1, ten).start()

        row_at = lax.broadcasted_iota(jnp.int32, (L, L), 0)
        col_at = lax.broadcasted_iota(jnp.int32, (L, L), 1)
        causal = row_at >= col_at
        cos_t = cosine[...]
        sin_t = sine[...]

        def rotated(values):
            turned = pltpu.roll(values, head_dim // 2, 1)
            return (values * cos_t + turned * sin_t).astype(BF16)

        for h in range(heads):
            span = slice(h * head_dim, (h + 1) * head_dim)
            queries = rotated(acc[0, :, span] * scale)
            key_rows = rotated(acc[1, :, span] * scale)
            rate = mix[:, span]
            mixed = (
                rate * (acc[2, :, span] * scale) + (1.0 - rate) * fv[m, :, span].astype(F32)
            ).astype(BF16)
            scores = lax.dot_general(
                queries, key_rows, (((1,), (1,)), ((), ())), preferred_element_type=F32
            ) * head_dim ** (-0.5)
            scores = jnp.where(causal, scores, -1e30)
            expo = jnp.exp(scores - jnp.max(scores, axis=-1, keepdims=True))
            probs = (expo / jnp.sum(expo, axis=-1, keepdims=True)).astype(BF16)
            att[:, span] = jnp.dot(probs, mixed, preferred_element_type=F32).astype(BF16)

        @pl.when(m == 0)
        def _():
            loads[3].wait()

        attended = att[...]
        order = list(range(1, Z)) + [0]

        def projected(t):
            span = pl.ds(pl.multiple_of(t * W, W), W)
            return jnp.dot(attended, wo[:, span], preferred_element_type=F32).astype(BF16)

        for d in order:
            to_z = peer(d)
            part[m, to_z] = projected(2 * to_z + other)
            remote(
                part.at[m, to_z], sib.at[m, to_z], sp_s.at[m, to_z], sp_r.at[m, to_z], sec, mate
            ).start()
        total = full[m, ten].astype(F32)
        for d in order:
            to_z = peer(d)
            mine = projected(2 * to_z + c).astype(F32)
            arrived(sib.at[m, to_z], sp_s.at[m, to_z], sp_r.at[m, to_z])
            mine = mine + sib[m, to_z].astype(F32)
            if d == 0:
                total = total + mine
            else:
                pair[m, to_z] = mine.astype(BF16)
                remote(
                    pair.at[m, to_z], zr.at[m, z], zs_s.at[m, to_z], zs_r.at[m, z],
                    sec, 2 * to_z + c,
                ).start()
        for d in range(1, Z):
            from_z = peer(d)
            arrived(zr.at[m, from_z], zs_s.at[m, from_z], zs_r.at[m, from_z])
            total = total + zr[m, from_z].astype(F32)
        fresh = total.astype(BF16)
        out[0, m] = fresh
        hid[m] = fresh

        @pl.when(has_next)
        def _():
            for d in range(Z):
                remote(
                    hid.at[m], full.at[m, ten], hp_s.at[m, d], ag_r.at[m, z],
                    sec + 1, 2 * peer(d) + c,
                ).start()

        return carry

    lax.fori_loop(0, B, micro, 0)

    def drain(m, carry):
        for d in range(Z):
            at = peer(d)
            sent(full.at[m, 2 * at + c], fw_s.at[m, at], fw_r.at[m, at])
            sent(part.at[m, at], sp_s.at[m, at], sp_r.at[m, at])
            if d > 0:
                sent(pair.at[m, at], zs_s.at[m, at], zs_r.at[m, at])

        @pl.when(root)
        def _():
            for d in range(1, Z):
                sent(full.at[m, ten], ag_s.at[m, d], ag_r.at[m, z])

        @pl.when(sec > 0)
        def _():
            sent(looked.at[m], lk_s.at[m], lk_r.at[m, 0])

        @pl.when(has_next)
        def _():
            sent(fv.at[m], fv_s.at[m], fv_r.at[m])
            for d in range(Z):
                sent(hid.at[m], hp_s.at[m, d], ag_r.at[m, z])

        return carry

    lax.fori_loop(0, B, drain, 0)


def rotary_tables(length, head_dim):
    half_dim = head_dim // 2
    positions = jnp.arange(length, dtype=F32)
    frequency = ROTARY_BASE ** (-(jnp.arange(half_dim, dtype=F32) * 2.0) / head_dim)
    angles = positions[:, None] * frequency[None, :]
    cosine, sine = jnp.cos(angles), jnp.sin(angles)
    return jnp.concatenate([cosine, cosine], -1), jnp.concatenate([-sine, sine], -1)


def shards(
    sections, tensors,
    token_ids, emb_table, attn_gain, query_weight, key_weight, value_weight, mix_weight, out_weight,
):
    section_rank = lax.axis_index("section")
    batches, length = token_ids.shape
    vocab_local, width_local = emb_table.shape
    heads = mix_weight.shape[1]
    width = query_weight.shape[2]
    head_dim = width // heads
    features = query_weight.shape[1]
    flat_ids = token_ids.reshape(-1) - section_rank * vocab_local
    one_hot = (flat_ids[:, None] == jnp.arange(vocab_local, dtype=jnp.int32)[None, :]).astype(BF16)
    looked = jnp.dot(one_hot, emb_table, preferred_element_type=F32).astype(BF16)
    looked = looked.reshape(batches, length, width_local)
    cosine, sine = rotary_tables(length, head_dim)
    mix = jnp.repeat(mix_weight, head_dim, axis=1)
    S, T, B, L, W = sections, tensors, batches, length, width_local
    Z = T // 2
    vmem = pl.BlockSpec(memory_space=pltpu.VMEM)
    hbm = pl.BlockSpec(memory_space=pl.ANY)
    dma = pltpu.SemaphoreType.DMA
    blocks = pltpu.VMEM((B, Z, L, W), BF16)
    return pl.pallas_call(
        functools.partial(relay, (S, T, B, L, W, heads, head_dim)),
        out_shape=jax.ShapeDtypeStruct((1, B, L, W), BF16),
        in_specs=[vmem] * 5 + [hbm] * 4,
        out_specs=vmem,
        scratch_shapes=[
            pltpu.VMEM((features, width), BF16),
            pltpu.VMEM((features, width), BF16),
            pltpu.VMEM((features, width), BF16),
            pltpu.VMEM((width, features), BF16),
            pltpu.VMEM((B, max(S - 1, 1), L, W), BF16),
            pltpu.VMEM((B, T, L, W), BF16),
            pltpu.VMEM((B, L, width), BF16),
            blocks, blocks, blocks, blocks,
            pltpu.VMEM((B, L, W), BF16),
            pltpu.VMEM((3, L, width), F32),
            pltpu.VMEM((L, width), BF16),
            dma((4,)), dma((B,)), dma((B, S)),
            dma((B, Z)), dma((B, Z)), dma((B, Z)), dma((B, Z)),
            dma((B,)), dma((B,)),
            dma((B, Z)), dma((B, Z)), dma((B, Z)), dma((B, Z)), dma((B, Z)),
        ],
        compiler_params=pltpu.CompilerParams(
            collective_id=0, has_side_effects=True, vmem_limit_bytes=48 * 1024 * 1024
        ),
    )(looked, attn_gain.astype(F32), cosine, sine, mix, query_weight, key_weight, value_weight, out_weight)


def solution(mesh):
    in_specs = (
        P(),
        P("section", "tensor"),
        P("section", None),
        P("section", None, "tensor"),
        P("section", None, "tensor"),
        P("section", None, "tensor"),
        P("section", "tensor"),
        P("section", "tensor", None),
    )
    out_specs = P("section", None, None, "tensor")
    body = functools.partial(shards, mesh.shape["section"], mesh.shape["tensor"])
    return jax.shard_map(body, mesh=mesh, in_specs=in_specs, out_specs=out_specs, check_vma=False)
```

time: 539 us -> 108 us (0.20)
  waiting for transfers between devices: 318 us -> 0 us
  Pallas kernels: 0 us -> 100 us
  blocking collectives: 86.7 us -> 0 us
  matrix products: 86.3 us -> 4.89 us
  between operations: 13.2 us -> 0.04 us
  other arithmetic: 14.3 us -> 1.63 us
  starting transfers between devices: 7.89 us -> 0 us
  local copies, waits for them, and re-layouts: 8.01 us -> 1.48 us
    reduce_scatter x6 -> x0, waiting for transfers between devices: 179 us -> none  [advance(): lax.psum_scatter(attention_branch(full_rows, micro_index).astype(jnp.bflo...]
    pallas_call x0 -> x1, Pallas kernels: none -> 100 us  [shards(): pl.pallas_call(functools.partial(relay, (S, T, B, L, W, heads, head_dim))...]
    all_gather x6 -> x0, blocking collectives: 86.7 us -> none  [advance(): full_rows = lax.all_gather(shard_rows, 'tensor', axis=1, tiled=True)]
    psum x2 -> x0, waiting for transfers between devices: 85.7 us -> none  [the longest x1 42.9 us: broadcast(): return lax.psum(jnp.where(mine, array, jnp.zeros_like(array)), axis)]
    dot_general x31 -> x1, matrix products: 84.7 us -> 4.89 us  [shards(): jnp.dot(one_hot, emb_table, preferred_element_type=F32).astype(BF16)]
    ppermute x6 -> x0, waiting for transfers between devices: 28.1 us -> none  [shifted(): lax.ppermute(value, axis, [(source, source + steps) for source in range(f...]
    all_gather x1 -> x0, waiting for transfers between devices: 25.1 us -> none  [shards(): first_full = lax.all_gather(first_shard, 'tensor', axis=1, tiled=True)]
    ppermute x6 -> x0, starting transfers between devices: 7.75 us -> none  [shifted(): lax.ppermute(value, axis, [(source, source + steps) for source in range(f...]
  transfers between devices with their start and end apart: 15 -> 0, of which waited for: 15 -> 0; matrix products, arithmetic and copies ran while one was open for 0% -> 0% of each run, Pallas kernels for 0% -> 0%
where the time goes in v1:
time: 108 us
  Pallas kernels  100 us (93%)
  matrix products  4.89 us (5%)
  other arithmetic  1.63 us (2%)
  local copies, waits for them, and re-layouts  1.48 us (1%)
    pallas_call x1, Pallas kernels, shards(): pl.pallas_call(functools.partial(relay, (S, T, B, L, W, heads, head_dim))...  100 us
    dot_general x1, matrix products, shards(): jnp.dot(one_hot, emb_table, preferred_element_type=F32).astype(BF16)  4.89 us

profile of v1, /device:TPU:6, one launch (start us, length us, event | category | flops | bytes accessed | tf_op | source)
XLA Modules:
  0.0 108.1 jit_solution(18290464729035666445)
XLA Ops:
  0.0 0.7 broadcast_subtract_fusion
  0.7 0.1 sub.15
  0.8 0.7 broadcast_in_dim.4
  1.5 0.7 convert_element_type.8.gain
  2.2 0.1 fusion.5
  2.4 0.1 pad_maximum_fusion
  2.4 0.0 copy-start
  2.5 4.9 %fusion.2 = bf16[144,512]{1,0:T(8,128)(2,1)S(1)} fusion(bf16[8000,512]{1,0:T(8,128)(2,1)} %param.9, s32[144]{0:T(256)S(1)} %sub.15), kind=kOutput, calls=%fused_computation.3 | convolution fusion | flops 1180873728 | bytes 8340032 | tf_op jit(solution)/shard_map/dot_general | solution.py:283
  7.4 0.0 copy-done
  7.4 100.0 %shard_map.85 = bf16[1,3,48,512]{3,2,1,0:T(8,128)(2,1)S(1)} custom-call(bf16[3,48,512]{2,1,0:T(8,128)(2,1)S(1)} %bitcast.4, f32[1,4096]{1,0:T(1,128)S(1)} %convert_element_type.8.gain, f32[48,128]{1,0:T(8,128)S(1)} %get-tuple-element.8.cosine, f32[48,128]{1,0:T(8,128)S(1)} %get-tuple-element.9.sine, f32[1,512]{1,0:T(1,128)S(1)} %bitcast.5, ...), custom_call_target="tpu_custom_call" | custom-call | tf_op jit(solution)/shard_map/pallas_call | solution.py:293
  107.4 0.7 copy.10
  (1 shorter events, 0.0 us)
Async XLA Ops:
  2.4 4.9 %copy-start = (bf16[1,4096,512]{2,1,0:T(8,128)(2,1)S(1)}, bf16[1,4096,512]{2,1,0:T(8,128)(2,1)}, u32[]{:S(2)}) copy-start(bf16[1,4096,512]{2,1,0:T(8,128)(2,1)} %q_hbm.1) | copy-start | bytes 12582916

commit v2 on v1

v2 whole, which is shorter than its diff:
```python
import functools

import jax
import jax.numpy as jnp
import numpy as np
from jax import lax
from jax.experimental import pallas as pl
from jax.experimental.pallas import tpu as pltpu
from jax.sharding import PartitionSpec as P

EPSILON = 1e-05
ROTARY_BASE = 10000.0
MESH = pl.DeviceIdType.MESH
F32 = jnp.float32
BF16 = jnp.bfloat16


def relay(
    dims,
    looked, gain, cosine, sine, mix, q_hbm, k_hbm, v_hbm, o_hbm,
    out,
    wq, wk, wv, wo, lk, full, fv, part, sib, pair, zr, hid, acc, att, own, scales,
    w_sem, lk_s, lk_r, ag_s, ag_r, fw_s, fw_r, fv_s, fv_r, sp_s, sp_r, zs_s, zs_r, hp_s,
):
    S, T, B, C, L, W, heads, head_dim = dims
    Z = T // 2
    Wc = W // C
    sec = lax.axis_index("section")
    ten = lax.axis_index("tensor")
    z = lax.div(ten, 2)
    c = lax.rem(ten, 2)
    other = 1 - c
    mate = 2 * z + other
    root = sec == 0
    has_next = sec < S - 1

    def peer(d):
        return lax.rem(z + d, Z)

    def remote(src, dst, send, recv, to_sec, to_ten):
        return pltpu.make_async_remote_copy(
            src_ref=src, dst_ref=dst, send_sem=send, recv_sem=recv,
            device_id=(to_sec, to_ten), device_id_type=MESH,
        )

    def arrived(ref, send, recv):
        remote(ref, ref, send, recv, sec, mate).wait_recv()

    def sent(ref, send, recv):
        remote(ref, ref, send, recv, sec, mate).wait_send()

    loads = [
        pltpu.make_async_copy(hbm.at[0], vmem, w_sem.at[i])
        for i, (hbm, vmem) in enumerate(((q_hbm, wq), (k_hbm, wk), (v_hbm, wv), (o_hbm, wo)))
    ]
    for load in loads:
        load.start()

    barrier = pltpu.get_barrier_semaphore()

    def greet(to_sec, to_ten):
        pl.semaphore_signal(barrier, inc=1, device_id=(to_sec, to_ten), device_id_type=MESH)

    greet(sec, mate)
    for d in range(1, Z):
        greet(sec, 2 * peer(d) + c)

    @pl.when(has_next)
    def _():
        for d in range(Z):
            greet(sec + 1, 2 * peer(d) + c)

    @pl.when(sec > 0)
    def _():
        for d in range(Z):
            greet(sec - 1, 2 * peer(d) + c)
        greet(0, ten)

    @pl.when(root)
    def _():
        for s in range(1, S):
            greet(s, ten)

    greeted = Z + jnp.where(has_next, Z, 0) + jnp.where(root, S - 1, Z + 1)
    pl.semaphore_wait(barrier, greeted)

    @pl.when(sec > 0)
    def _():
        for m in range(B):
            remote(
                looked.at[m], lk.at[m, sec - 1], lk_s.at[m], lk_r.at[m, sec - 1], 0, ten
            ).start()

    @pl.when(root)
    def _():
        for m in range(B):
            rows = looked[m].astype(F32)
            for s in range(S - 1):
                arrived(lk.at[m, s], lk_s.at[m], lk_r.at[m, s])
                rows = rows + lk[m, s].astype(F32)
            for ch in range(C):
                full[m, ten, ch] = rows[:, ch * Wc:(ch + 1) * Wc].astype(BF16)
            for ch in range(C):
                for d in range(1, Z):
                    remote(
                        full.at[m, ten, ch], full.at[m, ten, ch],
                        ag_s.at[m, d, ch], ag_r.at[m, z, ch], sec, 2 * peer(d) + c,
                    ).start()

    for load in loads[:3]:
        load.wait()

    def project(m):
        def block(t, ch, square, first):
            rows = full[m, t, ch].astype(F32)
            span = pl.ds(pl.multiple_of(t * W + ch * Wc, Wc), Wc)
            scaled = (rows * gain[:, span].astype(F32)).astype(BF16)
            for i, weight in enumerate((wq, wk, wv)):
                product = jnp.dot(scaled, weight[span, :], preferred_element_type=F32)
                if first:
                    acc[i] = product
                else:
                    acc[i] += product
            return square + jnp.sum(rows * rows, axis=-1, keepdims=True)

        square = jnp.zeros((L, 1), F32)
        for ch in range(C):
            for d in range(Z):
                from_z = peer(d)
                t = 2 * from_z + c
                here = full.at[m, t, ch]

                def landed():
                    arrived(here, fw_s.at[m, from_z, ch], ag_r.at[m, from_z, ch])

                if d == 0:
                    pl.when(sec > 0)(landed)
                else:
                    landed()
                remote(
                    here, here, fw_s.at[m, from_z, ch], fw_r.at[m, from_z, ch], sec, mate
                ).start()
                square = block(t, ch, square, d == 0 and ch == 0)
        for ch in range(C):
            for d in range(Z):
                from_z = peer(d)
                t = 2 * from_z + other
                arrived(full.at[m, t, ch], fw_s.at[m, from_z, ch], fw_r.at[m, from_z, ch])
                square = block(t, ch, square, False)
        scale = lax.rsqrt(square * (1.0 / (T * W)) + EPSILON)
        scales[...] = jnp.broadcast_to(scale, scales.shape)

    order = list(range(1, Z)) + [0]

    def attend(m):
        scale = scales[...]

        @pl.when(root)
        def _():
            for h in range(heads):
                span = slice(h * head_dim, (h + 1) * head_dim)
                fv[m, :, span] = (acc[2, :, span] * scale).astype(BF16)

        @pl.when(sec > 0)
        def _():
            arrived(fv.at[m], fv_s.at[m], fv_r.at[m])

        @pl.when(has_next)
        def _():
            remote(fv.at[m], fv.at[m], fv_s.at[m], fv_r.at[m], sec + 1, ten).start()

        row_at = lax.broadcasted_iota(jnp.int32, (L, L), 0)
        col_at = lax.broadcasted_iota(jnp.int32, (L, L), 1)
        causal = row_at >= col_at
        cos_t = cosine[...]
        sin_t = sine[...]

        def rotated(values):
            turned = pltpu.roll(values, head_dim // 2, 1)
            return (values * cos_t + turned * sin_t).astype(BF16)

        for h in range(heads):
            span = slice(h * head_dim, (h + 1) * head_dim)
            queries = rotated(acc[0, :, span] * scale)
            key_rows = rotated(acc[1, :, span] * scale)
            rate = mix[0:1, h:h + 1]
            mixed = (
                rate * (acc[2, :, span] * scale) + (1.0 - rate) * fv[m, :, span].astype(F32)
            ).astype(BF16)
            scores = lax.dot_general(
                queries, key_rows, (((1,), (1,)), ((), ())), preferred_element_type=F32
            ) * head_dim ** (-0.5)
            scores = jnp.where(causal, scores, -1e30)
            expo = jnp.exp(scores - jnp.max(scores, axis=-1, keepdims=True))
            probs = (expo / jnp.sum(expo, axis=-1, keepdims=True)).astype(BF16)
            att[:, span] = jnp.dot(probs, mixed, preferred_element_type=F32).astype(BF16)

        @pl.when(m == 0)
        def _():
            loads[3].wait()

        attended = att[...]

        def projected(t, ch):
            span = pl.ds(pl.multiple_of(t * W + ch * Wc, Wc), Wc)
            return jnp.dot(attended, wo[:, span], preferred_element_type=F32).astype(BF16)

        for ch in range(C):
            for d in order:
                to_z = peer(d)
                part[m, to_z, ch] = projected(2 * to_z + other, ch)
                remote(
                    part.at[m, to_z, ch], sib.at[m, to_z, ch],
                    sp_s.at[m, to_z, ch], sp_r.at[m, to_z, ch], sec, mate,
                ).start()
        for ch in range(C):
            for d in order:
                to_z = peer(d)
                mine = projected(2 * to_z + c, ch).astype(F32)
                arrived(sib.at[m, to_z, ch], sp_s.at[m, to_z, ch], sp_r.at[m, to_z, ch])
                mine = mine + sib[m, to_z, ch].astype(F32)
                if d == 0:
                    own[ch] = full[m, ten, ch].astype(F32) + mine
                else:
                    pair[m, to_z, ch] = mine.astype(BF16)
                    remote(
                        pair.at[m, to_z, ch], zr.at[m, z, ch],
                        zs_s.at[m, to_z, ch], zs_r.at[m, z, ch], sec, 2 * to_z + c,
                    ).start()

    def finish(m):
        for ch in range(C):
            total = own[ch]
            for d in range(1, Z):
                from_z = peer(d)
                arrived(zr.at[m, from_z, ch], zs_s.at[m, from_z, ch], zs_r.at[m, from_z, ch])
                total = total + zr[m, from_z, ch].astype(F32)
            fresh = total.astype(BF16)
            hid[m, ch] = fresh

            @pl.when(has_next)
            def _():
                for d in range(Z):
                    remote(
                        hid.at[m, ch], full.at[m, ten, ch], hp_s.at[m, d, ch], ag_r.at[m, z, ch],
                        sec + 1, 2 * peer(d) + c,
                    ).start()

            out[0, m, :, ch * Wc:(ch + 1) * Wc] = fresh

    def step(m, carry):
        @pl.when(m < B)
        def _():
            project(m)

        @pl.when(m > 0)
        def _():
            finish(m - 1)

        @pl.when(m < B)
        def _():
            attend(m)

        return carry

    lax.fori_loop(0, B + 1, step, 0)

    def drain(m, carry):
        for ch in range(C):
            for d in range(Z):
                at = peer(d)
                sent(full.at[m, 2 * at + c, ch], fw_s.at[m, at, ch], fw_r.at[m, at, ch])
                sent(part.at[m, at, ch], sp_s.at[m, at, ch], sp_r.at[m, at, ch])
                if d > 0:
                    sent(pair.at[m, at, ch], zs_s.at[m, at, ch], zs_r.at[m, at, ch])

        @pl.when(root)
        def _():
            for ch in range(C):
                for d in range(1, Z):
                    sent(full.at[m, ten, ch], ag_s.at[m, d, ch], ag_r.at[m, z, ch])

        @pl.when(sec > 0)
        def _():
            sent(looked.at[m], lk_s.at[m], lk_r.at[m, 0])

        @pl.when(has_next)
        def _():
            sent(fv.at[m], fv_s.at[m], fv_r.at[m])
            for ch in range(C):
                for d in range(Z):
                    sent(hid.at[m, ch], hp_s.at[m, d, ch], ag_r.at[m, z, ch])

        return carry

    lax.fori_loop(0, B, drain, 0)


def rotary_tables(length, head_dim):
    half_dim = head_dim // 2
    positions = np.arange(length, dtype=np.float32)
    frequency = ROTARY_BASE ** (-(np.arange(half_dim, dtype=np.float64) * 2.0) / head_dim)
    angles = positions[:, None] * frequency.astype(np.float32)[None, :]
    cosine, sine = np.cos(angles), np.sin(angles)
    tables = np.concatenate([cosine, cosine], -1), np.concatenate([-sine, sine], -1)
    return tuple(jnp.asarray(table, F32) for table in tables)


def shards(
    sections, tensors,
    token_ids, emb_table, attn_gain, query_weight, key_weight, value_weight, mix_weight, out_weight,
):
    section_rank = lax.axis_index("section")
    batches, length = token_ids.shape
    vocab_local, width_local = emb_table.shape
    heads = mix_weight.shape[1]
    width = query_weight.shape[2]
    head_dim = width // heads
    features = query_weight.shape[1]
    flat_ids = token_ids.reshape(-1) - section_rank * vocab_local
    one_hot = (flat_ids[:, None] == jnp.arange(vocab_local, dtype=jnp.int32)[None, :]).astype(BF16)
    looked = jnp.dot(one_hot, emb_table, preferred_element_type=F32).astype(BF16)
    looked = looked.reshape(batches, length, width_local)
    cosine, sine = rotary_tables(length, head_dim)
    S, T, B, L, W = sections, tensors, batches, length, width_local
    Z = T // 2
    C = 2 if W % 256 == 0 else 1
    vmem = pl.BlockSpec(memory_space=pltpu.VMEM)
    hbm = pl.BlockSpec(memory_space=pl.ANY)
    dma = pltpu.SemaphoreType.DMA
    blocks = pltpu.VMEM((B, Z, C, L, W // C), BF16)
    return pl.pallas_call(
        functools.partial(relay, (S, T, B, C, L, W, heads, head_dim)),
        out_shape=jax.ShapeDtypeStruct((1, B, L, W), BF16),
        in_specs=[vmem] * 5 + [hbm] * 4,
        out_specs=vmem,
        scratch_shapes=[
            pltpu.VMEM((features, width), BF16),
            pltpu.VMEM((features, width), BF16),
            pltpu.VMEM((features, width), BF16),
            pltpu.VMEM((width, features), BF16),
            pltpu.VMEM((B, max(S - 1, 1), L, W), BF16),
            pltpu.VMEM((B, T, C, L, W // C), BF16),
            pltpu.VMEM((B, L, width), BF16),
            blocks, blocks, blocks, blocks,
            pltpu.VMEM((B, C, L, W // C), BF16),
            pltpu.VMEM((3, L, width), F32),
            pltpu.VMEM((L, width), BF16),
            pltpu.VMEM((C, L, W // C), F32),
            pltpu.VMEM((L, head_dim), F32),
            dma((4,)), dma((B,)), dma((B, S)),
            dma((B, Z, C)), dma((B, Z, C)), dma((B, Z, C)), dma((B, Z, C)),
            dma((B,)), dma((B,)),
            dma((B, Z, C)), dma((B, Z, C)), dma((B, Z, C)), dma((B, Z, C)), dma((B, Z, C)),
        ],
        compiler_params=pltpu.CompilerParams(
            collective_id=0, has_side_effects=True, vmem_limit_bytes=48 * 1024 * 1024
        ),
    )(looked, attn_gain, cosine, sine, mix_weight, query_weight, key_weight, value_weight, out_weight)


def solution(mesh):
    in_specs = (
        P(),
        P("section", "tensor"),
        P("section", None),
        P("section", None, "tensor"),
        P("section", None, "tensor"),
        P("section", None, "tensor"),
        P("section", "tensor"),
        P("section", "tensor", None),
    )
    out_specs = P("section", None, None, "tensor")
    body = functools.partial(shards, mesh.shape["section"], mesh.shape["tensor"])
    return jax.shard_map(body, mesh=mesh, in_specs=in_specs, out_specs=out_specs, check_vma=False)
```

time: 108 us -> 107 us (level)
  no operation moved by 1% of the time
where the time goes in v2:
time: 107 us
  Pallas kernels  100 us (93%)
  matrix products  4.89 us (5%)
    pallas_call x1, Pallas kernels, shards(): pl.pallas_call(functools.partial(relay, (S, T, B, C, L, W, heads, head_di...  100 us
    dot_general x1, matrix products, shards(): jnp.dot(one_hot, emb_table, preferred_element_type=F32).astype(BF16)  4.89 us

profile of v2, /device:TPU:6, one launch (start us, length us, event | category | flops | bytes accessed | tf_op | source)
XLA Modules:
  0.0 106.7 jit_solution(12060993536397490654)
XLA Ops:
  0.0 0.7 broadcast_subtract_fusion
  0.7 0.1 sub.15
  0.8 0.0 copy-start
  0.8 0.0 copy-start.1
  0.8 0.0 copy-start.2
  0.8 0.0 copy-start.3
  0.8 0.0 copy-start.4
  0.8 4.9 %fusion.2 = bf16[144,512]{1,0:T(8,128)(2,1)S(1)} fusion(bf16[8000,512]{1,0:T(8,128)(2,1)} %param.11, s32[144]{0:T(256)S(1)} %sub.15), kind=kOutput, calls=%fused_computation.3 | convolution fusion | flops 1180873728 | bytes 8340032 | tf_op jit(solution)/shard_map/dot_general | solution.py:322
  5.7 0.0 copy-done
  5.7 0.0 copy-done.1
  5.7 0.0 copy-done.2
  5.7 0.0 copy-done.3
  5.7 0.0 copy-done.4
  5.7 100.2 %shard_map.100 = bf16[1,3,48,512]{3,2,1,0:T(8,128)(2,1)S(1)} custom-call(bf16[3,48,512]{2,1,0:T(8,128)(2,1)S(1)} %bitcast.2, bf16[1,4096]{1,0:T(2,128)(2,1)S(1)} %copy-done.3, f32[48,128]{1,0:T(8,128)S(1)} %copy-done.2, f32[48,128]{1,0:T(8,128)S(1)} %copy-done.1, f32[1,4]{1,0:T(1,128)S(1)} %copy-done.4, bf16[1,4096,512]{2,1,0:T(8,128)(2,1)S(1)} %copy-done, ...), custom_call_target="tpu_custom_call" | custom-call | tf_op jit(solution)/shard_map/pallas_call | solution.py:332
  106.0 0.7 copy.12
Async XLA Ops:
  0.8 4.9 %copy-start = (bf16[1,4096,512]{2,1,0:T(8,128)(2,1)S(1)}, bf16[1,4096,512]{2,1,0:T(8,128)(2,1)}, u32[]{:S(2)}) copy-start(bf16[1,4096,512]{2,1,0:T(8,128)(2,1)} %q_hbm.1) | copy-start | bytes 12582916
  0.8 4.9 %copy-start.1 = (f32[48,128]{1,0:T(8,128)S(1)}, f32[48,128]{1,0:T(8,128)}, u32[]{:S(2)}) copy-start(f32[48,128]{1,0:T(8,128)} %constant.12.clone.sine) | copy-start | bytes 73732
  0.8 4.9 %copy-start.2 = (f32[48,128]{1,0:T(8,128)S(1)}, f32[48,128]{1,0:T(8,128)}, u32[]{:S(2)}) copy-start(f32[48,128]{1,0:T(8,128)} %constant.11.clone.cosine) | copy-start | bytes 73732
  0.8 5.0 %copy-start.3 = (bf16[1,4096]{1,0:T(2,128)(2,1)S(1)}, bf16[1,4096]{1,0:T(2,128)(2,1)}, u32[]{:S(2)}) copy-start(bf16[1,4096]{1,0:T(2,128)(2,1)} %gain.1) | copy-start | bytes 24580
  0.8 5.0 %copy-start.4 = (f32[1,4]{1,0:T(1,128)S(1)}, f32[1,4]{1,0:T(1,128)}, u32[]{:S(2)}) copy-start(f32[1,4]{1,0:T(1,128)} %mix.1) | copy-start | bytes 52
